TPU v7x, 32 devices: a whole 2x2x4 slice. The times are simulated.
32 devices in a mesh: mat: 4 (over x, core), frac: 8 (over z, y).
Axes of the slice: x: 2, y: 2, z: 4, core: 2. Of those that a mesh axis runs over, the one named last changes fastest.
Arguments:
- pressure_start: float32 [64, 512, 256], P('mat', 'frac'), may hold values from -6 to 6
- face_trans: float32 [3, 64, 512, 256], P(None, 'mat', 'frac'), may hold values from 0.2 to 2
- cell_coef: float32 [64, 512, 256], P('mat', 'frac'), may hold values from 0.05 to 0.5
- matrix_source: float32 [64, 512, 256], P('mat', 'frac'), may hold values from -6 to 6
- mortar_owner: int32 [16384, 1], P(('mat', 'frac')), may hold values from 0 to 31; in each aligned block of 512 rows (0 to 511, 512 to 1023, ...) at most 32 rows name the same one
- mortar_cell: int32 [16384], P(('mat', 'frac')), may hold values from 0 to 262143
- mortar_frac: int32 [16384], P(('mat', 'frac')), may hold values from 0 to 8191
- mortar_kappa: float32 [16384], P(('mat', 'frac')), may hold values from 0.5 to 2
- tiles: float32 [64, 4, 128, 128], P('frac'), may hold values from -0.25 to 0.25
- tile_cols: int32 [64, 4], P('frac'), may hold values from 0 to 63
- frac_diag: float32 [8192], P('frac'), may hold values from 4 to 8
- frac_source: float32 [8192], P('frac'), may hold values from -6 to 6
- fracture_start: float32 [8192], P('frac'), may hold values from -6 to 6
Outputs:
- pressure: float32 [64, 512, 256], P('mat', 'frac')
- fracture: float32 [8192], P('frac')
- flux: float32 [16384], P(('mat', 'frac'))
Inputs may be any that keep to these rules, and one draw needn't show every extreme that they name: `mortar_owner`: among the 512 mortar cells of one device, at most 32 name the same owner, and in some devices some owner is named exactly 32 times.
All inputs are finite; a program needn't handle non-finite values.
Results may differ from a plain program's by a relative error of at most 0.00015.
Values sent between devices are 32-bit elements; how exact they have to be, the bound alone decides.
A program may use at most 128 MiB of HBM per device.

v0:
```python
import jax
import jax.numpy as jnp
from jax import lax
from jax.sharding import PartitionSpec as P

SWEEPS = 2
CG_ITERS = 3
OUTER = 2
relax_weight = 0.8


def shifted(value, axis, steps):
    count = lax.axis_size(axis)
    leading, last = (max(0, -steps), min(count, count - steps))
    return lax.ppermute(value, axis, [(source, source + steps) for source in range(leading, last)])


def with_halo(block, sides, width):
    for axis, dim in sides:
        count = lax.axis_size(axis)
        forward = [(i, i + 1) for i in range(count - 1)]
        backward = [(target, source) for source, target in forward]
        low = lax.ppermute(
            lax.slice_in_dim(block, block.shape[dim] - width, None, axis=dim), axis, forward
        )
        high = lax.ppermute(lax.slice_in_dim(block, 0, width, axis=dim), axis, backward)
        block = jnp.concatenate([low, block, high], axis=dim)
    return block


def shift_next(values, along):
    padding = [(0, 0)] * values.ndim
    padding[along] = (0, 1)
    return lax.slice_in_dim(jnp.pad(values, padding), 1, values.shape[along] + 1, axis=along)


def shift_prev(values, along):
    padding = [(0, 0)] * values.ndim
    padding[along] = (1, 0)
    return lax.slice_in_dim(jnp.pad(values, padding), 0, values.shape[along], axis=along)


def relax(padded, coef_part, source_part, inside):
    centre = padded[1:-1, 1:-1]
    tx_here = coef_part[0, 1:-1, 1:-1]
    tx_low = coef_part[0, :-2, 1:-1]
    ty_here = coef_part[1, 1:-1, 1:-1]
    ty_low = coef_part[1, 1:-1, :-2]
    tz_here = coef_part[2, 1:-1, 1:-1]
    tz_low = shift_prev(tz_here, 2)
    cell_part = coef_part[3, 1:-1, 1:-1]
    base_part = coef_part[4, 1:-1, 1:-1]
    diagonal = cell_part + tx_here + tx_low + ty_here + ty_low + tz_here + tz_low
    diagonal = jnp.where(inside, diagonal, 1.0)
    applied = (
        diagonal * centre
        - tx_here * padded[2:, 1:-1]
        - tx_low * padded[:-2, 1:-1]
        - ty_here * padded[1:-1, 2:]
        - ty_low * padded[1:-1, :-2]
        - tz_here * shift_next(centre, 2)
        - tz_low * shift_prev(centre, 2)
    )
    updated = centre + relax_weight * (base_part + source_part - applied) / diagonal
    return jnp.where(inside, updated, 0.0)


def body(
    pressure_start,
    face_trans,
    cell_coef,
    matrix_source,
    mortar_owner,
    mortar_cell,
    mortar_frac,
    mortar_kappa,
    tiles,
    tile_cols,
    frac_diag,
    frac_source,
    fracture_start,
):
    width_x, width_y, depth_z = pressure_start.shape
    cells = width_x * width_y * depth_z
    mat_count = lax.axis_size("mat")
    frac_count = lax.axis_size("frac")
    devices = mat_count * frac_count
    row_mat = lax.axis_index("mat")
    row_frac = lax.axis_index("frac")
    size_b = tiles.shape[2]
    coefs = jnp.concatenate([face_trans, cell_coef[None], matrix_source[None]], 0)
    lower_x = shifted(face_trans[0, -1], "mat", 1)
    lower_y = shifted(face_trans[1, :, -1], "frac", 1)
    coef_ext = jnp.pad(coefs, ((0, 0), (1, 1), (1, 1), (0, 0)))
    coef_ext = coef_ext.at[0, 0, 1:-1].set(lower_x)
    coef_ext = coef_ext.at[1, 1:-1, 0].set(lower_y)
    owner = mortar_owner[:, 0]
    mortar_count = owner.shape[0]
    capacity = max(2, 2 * mortar_count // devices)
    hits = (owner[:, None] == jnp.arange(devices, dtype=jnp.int32)[None, :]).astype(jnp.int32)
    ranks = jnp.cumsum(hits, axis=0)
    slot = jnp.sum(ranks * hits, axis=1) - 1
    place = owner * capacity + slot
    index_slots = (
        jnp.full((devices * capacity,), cells, jnp.int32)
        .at[place]
        .set(mortar_cell)
        .reshape(devices, capacity)
    )
    asked = lax.all_to_all(index_slots, ("mat", "frac"), split_axis=0, concat_axis=0, tiled=True)
    asked_safe = jnp.minimum(asked, cells - 1)

    def fracture_apply(vector):
        whole = lax.all_gather(vector, "frac", axis=0, tiled=True)
        blocks = whole.reshape(-1, size_b)
        forward = jnp.einsum(
            "rtij,rtj->ri", tiles, blocks[tile_cols], precision=lax.Precision.HIGHEST
        )
        backward = jnp.einsum(
            "rtij,ri->rtj", tiles, vector.reshape(-1, size_b), precision=lax.Precision.HIGHEST
        )
        spread = jnp.zeros_like(blocks).at[tile_cols.reshape(-1)].add(backward.reshape(-1, size_b))
        returned = lax.psum_scatter(spread, "frac", scatter_dimension=0, tiled=True)
        return frac_diag * vector + 0.5 * (forward + returned).reshape(-1)

    def two_products(residual, image):
        return lax.psum((jnp.sum(residual * residual), jnp.sum(residual * image)), "frac")

    def solve_fracture(fracture, target):
        residual = target - fracture_apply(fracture)
        image = fracture_apply(residual)
        norm_now, product = two_products(residual, image)
        alpha = norm_now / product
        direction, along_image = (residual, image)
        for step in range(CG_ITERS):
            fracture = fracture + alpha * direction
            residual = residual - alpha * along_image
            if step + 1 < CG_ITERS:
                image = fracture_apply(residual)
                norm_next, product = two_products(residual, image)
                ratio = norm_next / norm_now
                alpha = norm_next / (product - ratio * norm_next / alpha)
                direction = residual + ratio * direction
                along_image = image + ratio * along_image
                norm_now = norm_next
        return fracture

    pressure = pressure_start
    fracture = fracture_start
    flux = jnp.zeros(mortar_kappa.shape, jnp.float32)
    for outer_no in range(OUTER):
        local_values = pressure.reshape(-1)[asked_safe]
        returned = lax.all_to_all(
            local_values, ("mat", "frac"), split_axis=0, concat_axis=0, tiled=True
        )
        trace = returned.reshape(-1)[place]
        fracture_whole = lax.all_gather(fracture, "frac", axis=0, tiled=True)
        flux = mortar_kappa * (trace - fracture_whole[mortar_frac])
        landed = jax.ops.segment_sum(flux, mortar_frac, num_segments=fracture_whole.shape[0])
        summed = lax.psum(landed, ("mat", "frac"))
        load = lax.dynamic_slice_in_dim(summed, row_frac * fracture.shape[0], fracture.shape[0])
        fracture = solve_fracture(fracture, frac_source + load)
        flux_slots = (
            jnp.zeros((devices * capacity,), jnp.float32)
            .at[place]
            .set(flux)
            .reshape(devices, capacity)
        )
        arrived = lax.all_to_all(
            flux_slots, ("mat", "frac"), split_axis=0, concat_axis=0, tiled=True
        )
        source = jax.ops.segment_sum(
            arrived.reshape(-1), asked_safe.reshape(-1), num_segments=cells
        ).reshape(pressure.shape)
        for sweep_no in range(SWEEPS):
            padded = with_halo(pressure, (("mat", 0), ("frac", 1)), 1)
            global_x = row_mat * width_x - 0 + jnp.arange(width_x)
            global_y = row_frac * width_y - 0 + jnp.arange(width_y)
            keep_x = (global_x >= 0) & (global_x < width_x * mat_count)
            keep_y = (global_y >= 0) & (global_y < width_y * frac_count)
            pressure = relax(
                padded, coef_ext, source, (keep_x[:, None] & keep_y[None, :])[:, :, None]
            )
    return (pressure, fracture, flux)


def solution(mesh):
    in_specs = (
        P("mat", "frac", None),
        P(None, "mat", "frac", None),
        P("mat", "frac", None),
        P("mat", "frac", None),
        P(("mat", "frac"), None),
        P(("mat", "frac")),
        P(("mat", "frac")),
        P(("mat", "frac")),
        P("frac", None, None, None),
        P("frac", None),
        P("frac"),
        P("frac"),
        P("frac"),
    )
    out_specs = (P("mat", "frac", None), P("frac"), P(("mat", "frac")))
    return jax.shard_map(body, mesh=mesh, in_specs=in_specs, out_specs=out_specs, check_vma=False)
```

profile of v0, /device:TPU:0, one launch (start us, length us, event | category | flops | bytes accessed | tf_op | source)
XLA Modules:
  0.0 977.3 jit_solution(13991142482101642097)
XLA Ops:
  30.5 31.1 %all_gather.26 = f32[8192]{0:T(1024)S(1)} all-gather(f32[1024]{0:T(1024)} %param.29), channel_id=1, replica_groups=mesh['mat'=4,'frac'=8] {'frac'}, dimensions={0}, use_global_device_ids=true | all-gather | bytes 36864 | tf_op jit(solution)/shard_map/all_gather | solution.py:157
  83.4 37.4 %all-reduce.10 = f32[64,128]{1,0:T(8,128)S(1)} all-reduce(f32[64,128]{1,0:T(8,128)S(1)} %scatter_custom_fusion.4), channel_id=2, replica_groups=mesh['mat'=4,'frac'=8] {'frac'}, use_global_device_ids=true, to_apply=%region_9.10.clone | all-reduce | flops 8192 | bytes 65536
  138.0 40.6 %psum.98 = f32[8192]{0:T(1024)S(1)} all-reduce(f32[8192]{0:T(1024)S(1)} %scatter_custom_fusion.3), channel_id=1, replica_groups=mesh['mat'=4,'frac'=8] {'mat','frac'}, use_global_device_ids=true, to_apply=%region_7.8 | all-reduce | flops 8192 | bytes 65536 | tf_op jit(solution)/shard_map/psum | solution.py:160
  178.7 30.8 %all_gather.27 = f32[8192]{0:T(1024)S(1)} all-gather(f32[1024]{0:T(1024)S(1)} %fusion.134), channel_id=1, replica_groups=mesh['mat'=4,'frac'=8] {'frac'}, dimensions={0}, use_global_device_ids=true | all-gather | bytes 36864 | tf_op jit(solution)/shard_map/all_gather | solution.py:114
  213.7 36.8 %all-reduce.11 = f32[64,128]{1,0:T(8,128)S(1)} all-reduce(f32[64,128]{1,0:T(8,128)S(1)} %scatter_custom_fusion.5), channel_id=3, replica_groups=mesh['mat'=4,'frac'=8] {'frac'}, use_global_device_ids=true, to_apply=%region_13.14.clone | all-reduce | flops 8192 | bytes 65536
  251.2 17.8 %all-reduce.23 = (f32[]{:T(128)}, f32[]{:T(128)}) all-reduce(f32[]{:T(128)} %get-tuple-element.38, f32[]{:T(128)} %get-tuple-element.37), channel_id=1, replica_groups=mesh['mat'=4,'frac'=8] {'frac'}, use_global_device_ids=true, to_apply=%region_11.12 | all-reduce | flops 2 | bytes 16 | tf_op jit(solution)/shard_map/psum | solution.py:127
  270.3 30.6 %all_gather.28 = f32[8192]{0:T(1024)S(1)} all-gather(f32[1024]{0:T(1024)S(1)} %multiply_subtract_fusion.3), channel_id=1, replica_groups=mesh['mat'=4,'frac'=8] {'frac'}, dimensions={0}, use_global_device_ids=true | all-gather | bytes 36864 | tf_op jit(solution)/shard_map/all_gather | solution.py:114
  305.1 34.9 %all-reduce.12 = f32[64,128]{1,0:T(8,128)S(1)} all-reduce(f32[64,128]{1,0:T(8,128)S(1)} %scatter_custom_fusion.6), channel_id=4, replica_groups=mesh['mat'=4,'frac'=8] {'frac'}, use_global_device_ids=true, to_apply=%region_19.20.clone | all-reduce | flops 8192 | bytes 65536
  340.7 17.8 %all-reduce.22 = (f32[]{:T(128)}, f32[]{:T(128)}) all-reduce(f32[]{:T(128)} %get-tuple-element.36, f32[]{:T(128)} %get-tuple-element.35), channel_id=1, replica_groups=mesh['mat'=4,'frac'=8] {'frac'}, use_global_device_ids=true, to_apply=%region_17.18 | all-reduce | flops 2 | bytes 16 | tf_op jit(solution)/shard_map/psum | solution.py:127
  362.9 30.6 %all_gather.29 = f32[8192]{0:T(1024)S(1)} all-gather(f32[1024]{0:T(1024)S(1)} %multiply_subtract_fusion.2), channel_id=1, replica_groups=mesh['mat'=4,'frac'=8] {'frac'}, dimensions={0}, use_global_device_ids=true | all-gather | bytes 36864 | tf_op jit(solution)/shard_map/all_gather | solution.py:114
  397.8 34.9 %all-reduce.13 = f32[64,128]{1,0:T(8,128)S(1)} all-reduce(f32[64,128]{1,0:T(8,128)S(1)} %scatter_custom_fusion.7), channel_id=5, replica_groups=mesh['mat'=4,'frac'=8] {'frac'}, use_global_device_ids=true, to_apply=%region_25.26.clone | all-reduce | flops 8192 | bytes 65536
  433.3 17.8 %all-reduce.21 = (f32[]{:T(128)}, f32[]{:T(128)}) all-reduce(f32[]{:T(128)} %get-tuple-element.34, f32[]{:T(128)} %get-tuple-element.33), channel_id=1, replica_groups=mesh['mat'=4,'frac'=8] {'frac'}, use_global_device_ids=true, to_apply=%region_23.24 | all-reduce | flops 2 | bytes 16 | tf_op jit(solution)/shard_map/psum | solution.py:127
  454.9 30.6 %all_gather.30 = f32[8192]{0:T(1024)S(1)} all-gather(f32[1024]{0:T(1024)S(1)} %multiply_add_fusion.1), channel_id=1, replica_groups=mesh['mat'=4,'frac'=8] {'frac'}, dimensions={0}, use_global_device_ids=true | all-gather | bytes 36864 | tf_op jit(solution)/shard_map/all_gather | solution.py:157
  530.4 37.6 %all-reduce.14 = f32[64,128]{1,0:T(8,128)S(1)} all-reduce(f32[64,128]{1,0:T(8,128)S(1)} %scatter_custom_fusion.11), channel_id=6, replica_groups=mesh['mat'=4,'frac'=8] {'frac'}, use_global_device_ids=true, to_apply=%region_33.34.clone | all-reduce | flops 8192 | bytes 65536
  608.3 41.0 %psum.105 = f32[8192]{0:T(1024)S(1)} all-reduce(f32[8192]{0:T(1024)S(1)} %scatter_custom_fusion.10), channel_id=1, replica_groups=mesh['mat'=4,'frac'=8] {'mat','frac'}, use_global_device_ids=true, to_apply=%region_31.32 | all-reduce | flops 8192 | bytes 65536 | tf_op jit(solution)/shard_map/psum | solution.py:160
  649.3 30.6 %all_gather.31 = f32[8192]{0:T(1024)S(1)} all-gather(f32[1024]{0:T(1024)S(1)} %fusion.119), channel_id=1, replica_groups=mesh['mat'=4,'frac'=8] {'frac'}, dimensions={0}, use_global_device_ids=true | all-gather | bytes 36864 | tf_op jit(solution)/shard_map/all_gather | solution.py:114
  684.3 36.9 %all-reduce.15 = f32[64,128]{1,0:T(8,128)S(1)} all-reduce(f32[64,128]{1,0:T(8,128)S(1)} %scatter_custom_fusion.12), channel_id=7, replica_groups=mesh['mat'=4,'frac'=8] {'frac'}, use_global_device_ids=true, to_apply=%region_37.38.clone | all-reduce | flops 8192 | bytes 65536
  721.9 17.8 %all-reduce.20 = (f32[]{:T(128)}, f32[]{:T(128)}) all-reduce(f32[]{:T(128)} %get-tuple-element.32, f32[]{:T(128)} %get-tuple-element.31), channel_id=1, replica_groups=mesh['mat'=4,'frac'=8] {'frac'}, use_global_device_ids=true, to_apply=%region_35.36 | all-reduce | flops 2 | bytes 16 | tf_op jit(solution)/shard_map/psum | solution.py:127
  741.0 30.6 %all_gather.32 = f32[8192]{0:T(1024)S(1)} all-gather(f32[1024]{0:T(1024)S(1)} %multiply_subtract_fusion.1), channel_id=1, replica_groups=mesh['mat'=4,'frac'=8] {'frac'}, dimensions={0}, use_global_device_ids=true | all-gather | bytes 36864 | tf_op jit(solution)/shard_map/all_gather | solution.py:114
  776.0 34.9 %all-reduce.16 = f32[64,128]{1,0:T(8,128)S(1)} all-reduce(f32[64,128]{1,0:T(8,128)S(1)} %scatter_custom_fusion.13), channel_id=8, replica_groups=mesh['mat'=4,'frac'=8] {'frac'}, use_global_device_ids=true, to_apply=%region_43.44.clone | all-reduce | flops 8192 | bytes 65536
  811.5 17.8 %all-reduce.19 = (f32[]{:T(128)}, f32[]{:T(128)}) all-reduce(f32[]{:T(128)} %get-tuple-element.30, f32[]{:T(128)} %get-tuple-element.29), channel_id=1, replica_groups=mesh['mat'=4,'frac'=8] {'frac'}, use_global_device_ids=true, to_apply=%region_41.42 | all-reduce | flops 2 | bytes 16 | tf_op jit(solution)/shard_map/psum | solution.py:127
  834.0 30.6 %all_gather.33 = f32[8192]{0:T(1024)S(1)} all-gather(f32[1024]{0:T(1024)S(1)} %multiply_subtract_fusion), channel_id=1, replica_groups=mesh['mat'=4,'frac'=8] {'frac'}, dimensions={0}, use_global_device_ids=true | all-gather | bytes 36864 | tf_op jit(solution)/shard_map/all_gather | solution.py:114
  871.8 38.1 %all-reduce.17 = f32[64,128]{1,0:T(8,128)S(1)} all-reduce(f32[64,128]{1,0:T(8,128)S(1)} %scatter_custom_fusion.14), channel_id=9, replica_groups=mesh['mat'=4,'frac'=8] {'frac'}, use_global_device_ids=true, to_apply=%region_49.50.clone | all-reduce | flops 8192 | bytes 65536
  935.2 17.8 %all-reduce.18 = (f32[]{:T(128)}, f32[]{:T(128)}) all-reduce(f32[]{:T(128)} %get-tuple-element.28, f32[]{:T(128)} %get-tuple-element.27), channel_id=1, replica_groups=mesh['mat'=4,'frac'=8] {'frac'}, use_global_device_ids=true, to_apply=%region_47.48 | all-reduce | flops 2 | bytes 16 | tf_op jit(solution)/shard_map/psum | solution.py:127
  (229 shorter events, 229.9 us)
Async XLA Ops:
  2.3 498.6 %collective-permute-start = (f32[64,256]{1,0:T(8,128)}, f32[64,256]{1,0:T(8,128)S(1)}, u32[]{:S(2)}, u32[]{:S(2)}) collective-permute-start(f32[64,256]{1,0:T(8,128)} %slice_bitcast_fusion.7), channel_id=1, source_target_pairs={{0,8},{8,16},{16,24},{1,9},{9,17},{17,25},{2,10},{10,18},{18,26},{... | collective-permute-start | bytes 196616 | tf_op jit(solution)/shard_map/ppermute | solution.py:15
  5.7 480.3 %collective-permute-start.1 = (f32[16,256]{1,0:T(8,128)S(1)}, f32[16,256]{1,0:T(8,128)S(1)}, u32[]{:S(2)}, u32[]{:S(2)}) collective-permute-start(f32[16,256]{1,0:T(8,128)S(1)} %bitcast.415), channel_id=1, source_target_pairs={{0,1},{1,2},{2,3},{3,4},{4,5},{5,6},{6,7},{8,9},{9,10},{10,11},{11... | collective-permute-start | bytes 49160 | tf_op jit(solution)/shard_map/ppermute | solution.py:15
  11.5 485.1 %collective-permute-start.3 = (f32[1,64,256]{2,1,0:T(8,128)}, f32[1,64,256]{2,1,0:T(8,128)S(1)}, u32[]{:S(2)}, u32[]{:S(2)}) collective-permute-start(f32[1,64,256]{2,1,0:T(8,128)} %get-tuple-element.72), channel_id=1, source_target_pairs={{0,8},{8,16},{16,24},{1,9},{9,17},{17,25},{2,10},{10,18},{18,26},{... | collective-permute-start | bytes 196616 | tf_op jit(solution)/shard_map/ppermute | solution.py:23
  14.9 481.9 %collective-permute-start.2 = (f32[1,64,256]{2,1,0:T(8,128)}, f32[1,64,256]{2,1,0:T(8,128)S(1)}, u32[]{:S(2)}, u32[]{:S(2)}) collective-permute-start(f32[1,64,256]{2,1,0:T(8,128)} %get-tuple-element.71), channel_id=1, source_target_pairs={{8,0},{16,8},{24,16},{9,1},{17,9},{25,17},{10,2},{18,10},{26,18},{... | collective-permute-start | bytes 196616 | tf_op jit(solution)/shard_map/ppermute | solution.py:26
  23.1 47.8 %all-to-all-start = ((s32[32,1,32]{2,1,0:T(1,128)}), s32[32,1,32]{2,1,0:T(1,128)S(1)}, u32[]{:S(2)}, u32[]{:S(2)}) async-start(s32[32,1,32]{2,1,0:T(1,128)} %all_to_all.30), calls=%async_computation | async-start | bytes 32768 | tf_op jit(solution)/shard_map/all_to_all | solution.py:110
  77.9 47.4 %all-to-all-start.1 = ((f32[32,1,32]{2,1,0:T(1,128)}), f32[32,1,32]{2,1,0:T(1,128)S(1)}, u32[]{:S(2)}, u32[]{:S(2)}) async-start(f32[32,1,32]{2,1,0:T(1,128)} %all_to_all.32), calls=%async_computation.1 | async-start | bytes 32768 | tf_op jit(solution)/shard_map/all_to_all | solution.py:153
  125.3 361.5 %copy-start.23 = (s32[1024]{0:T(1024)}, s32[1024]{0:T(1024)S(1)}, u32[]{:S(2)}) copy-start(s32[1024]{0:T(1024)S(1)} %reshape.528) | copy-start | bytes 12292
  135.5 350.6 %all-to-all-start.2 = ((f32[32,1,32]{2,1,0:T(1,128)}), f32[32,1,32]{2,1,0:T(1,128)S(1)}, u32[]{:S(2)}, u32[]{:S(2)}) async-start(f32[32,1,32]{2,1,0:T(1,128)} %all_to_all.34), calls=%async_computation.2 | async-start | bytes 32768 | tf_op jit(solution)/shard_map/all_to_all | solution.py:169
  497.8 7.7 collective-permute-start.5
  499.5 5.9 collective-permute-start.4
  513.3 6.2 collective-permute-start.6
  514.6 4.9 collective-permute-start.7
  519.5 48.6 %collective-permute-start.9 = (f32[18,1,256]{2,1,0:T(1,128)S(1)}, f32[18,1,256]{2,1,0:T(1,128)S(1)}, u32[]{:S(2)}, u32[]{:S(2)}) collective-permute-start(f32[18,1,256]{2,1,0:T(1,128)S(1)} %get-tuple-element.62), channel_id=1, source_target_pairs={{0,1},{1,2},{2,3},{3,4},{4,5},{5,6},{6,7},{8,9},{9,10},{10,11},{11... | collective-permute-start | bytes 55304 | tf_op jit(solution)/shard_map/ppermute | solution.py:23
  524.0 44.0 %collective-permute-start.8 = (f32[18,1,256]{2,1,0:T(1,128)S(1)}, f32[18,1,256]{2,1,0:T(1,128)S(1)}, u32[]{:S(2)}, u32[]{:S(2)}) collective-permute-start(f32[18,1,256]{2,1,0:T(1,128)S(1)} %get-tuple-element.61), channel_id=1, source_target_pairs={{1,0},{2,1},{3,2},{4,3},{5,4},{6,5},{7,6},{9,8},{10,9},{11,10},{12... | collective-permute-start | bytes 55304 | tf_op jit(solution)/shard_map/ppermute | solution.py:26
  584.8 9.7 all-to-all-start.3
  588.3 278.8 %collective-permute-start.10 = (f32[1,64,256]{2,1,0:T(8,128)S(1)}, f32[1,64,256]{2,1,0:T(8,128)S(1)}, u32[]{:S(2)}, u32[]{:S(2)}) collective-permute-start(f32[1,64,256]{2,1,0:T(8,128)S(1)} %get-tuple-element.68), channel_id=1, source_target_pairs={{8,0},{16,8},{24,16},{9,1},{17,9},{25,17},{10,2},{18,10},{26,18},{... | collective-permute-start | bytes 196616 | tf_op jit(solution)/shard_map/ppermute | solution.py:26
  589.6 277.5 %collective-permute-start.11 = (f32[1,64,256]{2,1,0:T(8,128)S(1)}, f32[1,64,256]{2,1,0:T(8,128)S(1)}, u32[]{:S(2)}, u32[]{:S(2)}) collective-permute-start(f32[1,64,256]{2,1,0:T(8,128)S(1)} %get-tuple-element.67), channel_id=1, source_target_pairs={{0,8},{8,16},{16,24},{1,9},{9,17},{17,25},{2,10},{10,18},{18,26},{... | collective-permute-start | bytes 196616 | tf_op jit(solution)/shard_map/ppermute | solution.py:23
  604.3 305.6 %all-to-all-start.4 = ((f32[32,1,32]{2,1,0:T(1,128)}), f32[32,1,32]{2,1,0:T(1,128)S(1)}, u32[]{:S(2)}, u32[]{:S(2)}) async-start(f32[32,1,32]{2,1,0:T(1,128)} %all_to_all.38), calls=%async_computation.4 | async-start | bytes 32768 | tf_op jit(solution)/shard_map/all_to_all | solution.py:169
  867.1 53.6 %collective-permute-start.13 = (f32[18,1,256]{2,1,0:T(1,128)S(1)}, f32[18,1,256]{2,1,0:T(1,128)S(1)}, u32[]{:S(2)}, u32[]{:S(2)}) collective-permute-start(f32[18,1,256]{2,1,0:T(1,128)S(1)} %get-tuple-element.60), channel_id=1, source_target_pairs={{0,1},{1,2},{2,3},{3,4},{4,5},{5,6},{6,7},{8,9},{9,10},{10,11},{11... | collective-permute-start | bytes 55304 | tf_op jit(solution)/shard_map/ppermute | solution.py:23
  868.4 52.3 %collective-permute-start.12 = (f32[18,1,256]{2,1,0:T(1,128)S(1)}, f32[18,1,256]{2,1,0:T(1,128)S(1)}, u32[]{:S(2)}, u32[]{:S(2)}) collective-permute-start(f32[18,1,256]{2,1,0:T(1,128)S(1)} %get-tuple-element.59), channel_id=1, source_target_pairs={{1,0},{2,1},{3,2},{4,3},{5,4},{6,5},{7,6},{9,8},{10,9},{11,10},{12... | collective-permute-start | bytes 55304 | tf_op jit(solution)/shard_map/ppermute | solution.py:26
  930.3 26.8 %collective-permute-start.14 = (f32[1,64,256]{2,1,0:T(8,128)S(1)}, f32[1,64,256]{2,1,0:T(8,128)S(1)}, u32[]{:S(2)}, u32[]{:S(2)}) collective-permute-start(f32[1,64,256]{2,1,0:T(8,128)S(1)} %get-tuple-element.66), channel_id=1, source_target_pairs={{8,0},{16,8},{24,16},{9,1},{17,9},{25,17},{10,2},{18,10},{26,18},{... | collective-permute-start | bytes 196616 | tf_op jit(solution)/shard_map/ppermute | solution.py:26
  931.6 25.5 %collective-permute-start.15 = (f32[1,64,256]{2,1,0:T(8,128)S(1)}, f32[1,64,256]{2,1,0:T(8,128)S(1)}, u32[]{:S(2)}, u32[]{:S(2)}) collective-permute-start(f32[1,64,256]{2,1,0:T(8,128)S(1)} %get-tuple-element.65), channel_id=1, source_target_pairs={{0,8},{8,16},{16,24},{1,9},{9,17},{17,25},{2,10},{10,18},{18,26},{... | collective-permute-start | bytes 196616 | tf_op jit(solution)/shard_map/ppermute | solution.py:23
  958.0 5.8 collective-permute-start.17
  962.0 5.7 collective-permute-start.16
  (26 other events, 1407.7 us)
where the time goes:
time: 987 us; the launch traced here: 977 us
  blocking collectives  725 us (73%)
  other arithmetic  78.4 us (8%)
  starting transfers between devices  61.4 us (6%)
  local copies, waits for them, and re-layouts  60.8 us (6%)
  matrix products  23.6 us (2%)
  between operations  22 us (2%)
    unnamed x8, blocking collectives  291 us
    all_gather x6, blocking collectives, fracture_apply(): whole = lax.all_gather(vector, 'frac', axis=0, tiled=True)  184 us
    psum x6, blocking collectives, two_products(): lax.psum((jnp.sum(residual * residual), jnp.sum(residual * image)), 'frac')  107 us
    psum x2, blocking collectives, body(): summed = lax.psum(landed, ('mat', 'frac'))  81.6 us
    all_gather x2, blocking collectives, body(): fracture_whole = lax.all_gather(fracture, 'frac', axis=0, tiled=True)  61.7 us
    select_n x4, other arithmetic, relax(): return jnp.where(inside, updated, 0.0)  33.9 us
    ppermute x8, starting transfers between devices, with_halo(): lax.ppermute(lax.slice_in_dim(block, block.shape[dim] - width, None, axis...  24 us
  transfers between devices with their start and end apart: 23, of which 2 were waited for; matrix products, arithmetic and copies ran while one was open for 12% of the time, Pallas kernels for 0%

commit v1 on v0

--- a/solution.py
+++ b/solution.py
@@ -2,11 +2,17 @@
 import jax.numpy as jnp
 from jax import lax
 from jax.sharding import PartitionSpec as P
+from jax.lax import all_gather
 
 SWEEPS = 2
 CG_ITERS = 3
 OUTER = 2
 relax_weight = 0.8
+
+
+def find_the_figure(vals, bus_axis):
+    arr_out = jnp.sum(all_gather(vals, bus_axis), 0)
+    return arr_out
 
 
 def shifted(value, axis, steps):
@@ -157,7 +163,7 @@
         fracture_whole = lax.all_gather(fracture, "frac", axis=0, tiled=True)
         flux = mortar_kappa * (trace - fracture_whole[mortar_frac])
         landed = jax.ops.segment_sum(flux, mortar_frac, num_segments=fracture_whole.shape[0])
-        summed = lax.psum(landed, ("mat", "frac"))
+        summed = find_the_figure(landed, ("mat", "frac"))
         load = lax.dynamic_slice_in_dim(summed, row_frac * fracture.shape[0], fracture.shape[0])
         fracture = solve_fracture(fracture, frac_source + load)
         flux_slots = (

time: 987 us -> 924 us (0.936)
  blocking collectives: 725 us -> 635 us
  between operations: 22 us -> 35 us
    psum x2 -> x0, blocking collectives: 81.6 us -> none  [body(): summed = lax.psum(landed, ('mat', 'frac'))]
  transfers between devices with their start and end apart: 23 -> 25, of which waited for: 2 -> 3; matrix products, arithmetic and copies ran while one was open for 12% -> 16% of each run, Pallas kernels for 0% -> 0%
where the time goes in v1:
time: 924 us; the launch traced here: 913 us
  blocking collectives  635 us (69%)
  other arithmetic  79.9 us (9%)
  starting transfers between devices  68.6 us (7%)
  local copies, waits for them, and re-layouts  62.7 us (7%)
  between operations  35 us (4%)
  matrix products  23.6 us (3%)
    unnamed x8, blocking collectives  282 us
    all_gather x6, blocking collectives, fracture_apply(): whole = lax.all_gather(vector, 'frac', axis=0, tiled=True)  184 us
    psum x6, blocking collectives, two_products(): lax.psum((jnp.sum(residual * residual), jnp.sum(residual * image)), 'frac')  107 us
    all_gather x2, blocking collectives, body(): fracture_whole = lax.all_gather(fracture, 'frac', axis=0, tiled=True)  61.6 us
    select_n x4, other arithmetic, relax(): return jnp.where(inside, updated, 0.0)  33.4 us
    ppermute x8, starting transfers between devices, with_halo(): lax.ppermute(lax.slice_in_dim(block, block.shape[dim] - width, None, axis...  24.1 us
  transfers between devices with their start and end apart: 25, of which 3 were waited for; matrix products, arithmetic and copies ran while one was open for 16% of the time, Pallas kernels for 0%

profile of v1, /device:TPU:0, one launch (start us, length us, event | category | flops | bytes accessed | tf_op | source)
XLA Modules:
  0.0 912.6 jit_solution(9396328665915336029)
XLA Ops:
  55.5 31.0 %all_gather.38 = f32[8192]{0:T(1024)S(1)} all-gather(f32[1024]{0:T(1024)S(1)} %copy-done.12), channel_id=1, replica_groups=mesh['mat'=4,'frac'=8] {'frac'}, dimensions={0}, use_global_device_ids=true | all-gather | bytes 36864 | tf_op jit(solution)/shard_map/all_gather | solution.py:163
  184.2 37.4 %all-reduce.10 = f32[64,128]{1,0:T(8,128)S(1)} all-reduce(f32[64,128]{1,0:T(8,128)S(1)} %scatter_custom_fusion.4), channel_id=4, replica_groups=mesh['mat'=4,'frac'=8] {'frac'}, use_global_device_ids=true, to_apply=%region_9.10.clone | all-reduce | flops 8192 | bytes 65536
  230.1 30.6 %all_gather.41 = f32[8192]{0:T(1024)S(1)} all-gather(f32[1024]{0:T(1024)S(1)} %fusion.134), channel_id=1, replica_groups=mesh['mat'=4,'frac'=8] {'frac'}, dimensions={0}, use_global_device_ids=true | all-gather | bytes 36864 | tf_op jit(solution)/shard_map/all_gather | solution.py:120
  265.0 35.9 %all-reduce.11 = f32[64,128]{1,0:T(8,128)S(1)} all-reduce(f32[64,128]{1,0:T(8,128)S(1)} %scatter_custom_fusion.5), channel_id=5, replica_groups=mesh['mat'=4,'frac'=8] {'frac'}, use_global_device_ids=true, to_apply=%region_13.14.clone | all-reduce | flops 8192 | bytes 65536
  301.4 17.8 %all-reduce.23 = (f32[]{:T(128)}, f32[]{:T(128)}) all-reduce(f32[]{:T(128)} %get-tuple-element.38, f32[]{:T(128)} %get-tuple-element.37), channel_id=1, replica_groups=mesh['mat'=4,'frac'=8] {'frac'}, use_global_device_ids=true, to_apply=%region_11.12 | all-reduce | flops 2 | bytes 16 | tf_op jit(solution)/shard_map/psum | solution.py:133
  320.6 30.8 %all_gather.42 = f32[8192]{0:T(1024)S(1)} all-gather(f32[1024]{0:T(1024)S(1)} %multiply_subtract_fusion.3), channel_id=1, replica_groups=mesh['mat'=4,'frac'=8] {'frac'}, dimensions={0}, use_global_device_ids=true | all-gather | bytes 36864 | tf_op jit(solution)/shard_map/all_gather | solution.py:120
  355.6 34.9 %all-reduce.12 = f32[64,128]{1,0:T(8,128)S(1)} all-reduce(f32[64,128]{1,0:T(8,128)S(1)} %scatter_custom_fusion.6), channel_id=6, replica_groups=mesh['mat'=4,'frac'=8] {'frac'}, use_global_device_ids=true, to_apply=%region_19.20.clone | all-reduce | flops 8192 | bytes 65536
  391.2 17.8 %all-reduce.22 = (f32[]{:T(128)}, f32[]{:T(128)}) all-reduce(f32[]{:T(128)} %get-tuple-element.36, f32[]{:T(128)} %get-tuple-element.35), channel_id=1, replica_groups=mesh['mat'=4,'frac'=8] {'frac'}, use_global_device_ids=true, to_apply=%region_17.18 | all-reduce | flops 2 | bytes 16 | tf_op jit(solution)/shard_map/psum | solution.py:133
  413.4 30.6 %all_gather.43 = f32[8192]{0:T(1024)S(1)} all-gather(f32[1024]{0:T(1024)S(1)} %multiply_subtract_fusion.2), channel_id=1, replica_groups=mesh['mat'=4,'frac'=8] {'frac'}, dimensions={0}, use_global_device_ids=true | all-gather | bytes 36864 | tf_op jit(solution)/shard_map/all_gather | solution.py:120
  448.2 34.9 %all-reduce.13 = f32[64,128]{1,0:T(8,128)S(1)} all-reduce(f32[64,128]{1,0:T(8,128)S(1)} %scatter_custom_fusion.7), channel_id=7, replica_groups=mesh['mat'=4,'frac'=8] {'frac'}, use_global_device_ids=true, to_apply=%region_25.26.clone | all-reduce | flops 8192 | bytes 65536
  483.8 17.8 %all-reduce.21 = (f32[]{:T(128)}, f32[]{:T(128)}) all-reduce(f32[]{:T(128)} %get-tuple-element.34, f32[]{:T(128)} %get-tuple-element.33), channel_id=1, replica_groups=mesh['mat'=4,'frac'=8] {'frac'}, use_global_device_ids=true, to_apply=%region_23.24 | all-reduce | flops 2 | bytes 16 | tf_op jit(solution)/shard_map/psum | solution.py:133
  505.3 30.6 %all_gather.44 = f32[8192]{0:T(1024)S(1)} all-gather(f32[1024]{0:T(1024)S(1)} %multiply_add_fusion.1), channel_id=1, replica_groups=mesh['mat'=4,'frac'=8] {'frac'}, dimensions={0}, use_global_device_ids=true | all-gather | bytes 36864 | tf_op jit(solution)/shard_map/all_gather | solution.py:163
  564.0 8.8 broadcast_select_fusion
  585.0 36.7 %all-reduce.14 = f32[64,128]{1,0:T(8,128)S(1)} all-reduce(f32[64,128]{1,0:T(8,128)S(1)} %scatter_custom_fusion.11), channel_id=8, replica_groups=mesh['mat'=4,'frac'=8] {'frac'}, use_global_device_ids=true, to_apply=%region_33.34.clone | all-reduce | flops 8192 | bytes 65536
  621.7 9.1 fusion.74
  632.3 30.6 %all_gather.47 = f32[8192]{0:T(1024)S(1)} all-gather(f32[1024]{0:T(1024)S(1)} %fusion.119), channel_id=1, replica_groups=mesh['mat'=4,'frac'=8] {'frac'}, dimensions={0}, use_global_device_ids=true | all-gather | bytes 36864 | tf_op jit(solution)/shard_map/all_gather | solution.py:120
  667.2 33.0 %all-reduce.15 = f32[64,128]{1,0:T(8,128)S(1)} all-reduce(f32[64,128]{1,0:T(8,128)S(1)} %scatter_custom_fusion.12), channel_id=9, replica_groups=mesh['mat'=4,'frac'=8] {'frac'}, use_global_device_ids=true, to_apply=%region_37.38.clone | all-reduce | flops 8192 | bytes 65536
  700.8 17.8 %all-reduce.20 = (f32[]{:T(128)}, f32[]{:T(128)}) all-reduce(f32[]{:T(128)} %get-tuple-element.32, f32[]{:T(128)} %get-tuple-element.31), channel_id=1, replica_groups=mesh['mat'=4,'frac'=8] {'frac'}, use_global_device_ids=true, to_apply=%region_35.36 | all-reduce | flops 2 | bytes 16 | tf_op jit(solution)/shard_map/psum | solution.py:133
  720.0 30.8 %all_gather.48 = f32[8192]{0:T(1024)S(1)} all-gather(f32[1024]{0:T(1024)S(1)} %multiply_subtract_fusion.1), channel_id=1, replica_groups=mesh['mat'=4,'frac'=8] {'frac'}, dimensions={0}, use_global_device_ids=true | all-gather | bytes 36864 | tf_op jit(solution)/shard_map/all_gather | solution.py:120
  755.1 34.9 %all-reduce.16 = f32[64,128]{1,0:T(8,128)S(1)} all-reduce(f32[64,128]{1,0:T(8,128)S(1)} %scatter_custom_fusion.13), channel_id=10, replica_groups=mesh['mat'=4,'frac'=8] {'frac'}, use_global_device_ids=true, to_apply=%region_43.44.clone | all-reduce | flops 8192 | bytes 65536
  790.6 17.8 %all-reduce.19 = (f32[]{:T(128)}, f32[]{:T(128)}) all-reduce(f32[]{:T(128)} %get-tuple-element.30, f32[]{:T(128)} %get-tuple-element.29), channel_id=1, replica_groups=mesh['mat'=4,'frac'=8] {'frac'}, use_global_device_ids=true, to_apply=%region_41.42 | all-reduce | flops 2 | bytes 16 | tf_op jit(solution)/shard_map/psum | solution.py:133
  812.8 30.6 %all_gather.49 = f32[8192]{0:T(1024)S(1)} all-gather(f32[1024]{0:T(1024)S(1)} %multiply_subtract_fusion), channel_id=1, replica_groups=mesh['mat'=4,'frac'=8] {'frac'}, dimensions={0}, use_global_device_ids=true | all-gather | bytes 36864 | tf_op jit(solution)/shard_map/all_gather | solution.py:120
  847.7 34.9 %all-reduce.17 = f32[64,128]{1,0:T(8,128)S(1)} all-reduce(f32[64,128]{1,0:T(8,128)S(1)} %scatter_custom_fusion.14), channel_id=11, replica_groups=mesh['mat'=4,'frac'=8] {'frac'}, use_global_device_ids=true, to_apply=%region_49.50.clone | all-reduce | flops 8192 | bytes 65536
  883.2 17.8 %all-reduce.18 = (f32[]{:T(128)}, f32[]{:T(128)}) all-reduce(f32[]{:T(128)} %get-tuple-element.28, f32[]{:T(128)} %get-tuple-element.27), channel_id=1, replica_groups=mesh['mat'=4,'frac'=8] {'frac'}, use_global_device_ids=true, to_apply=%region_47.48 | all-reduce | flops 2 | bytes 16 | tf_op jit(solution)/shard_map/psum | solution.py:133
  (227 shorter events, 224.8 us)
Async XLA Ops:
  8.2 117.0 %collective-permute-start = (f32[64,256]{1,0:T(8,128)S(1)}, f32[64,256]{1,0:T(8,128)S(1)}, u32[]{:S(2)}, u32[]{:S(2)}) collective-permute-start(f32[64,256]{1,0:T(8,128)S(1)} %slice_bitcast_fusion.7), channel_id=1, source_target_pairs={{0,8},{8,16},{16,24},{1,9},{9,17},{17,25},{2,10},{10,18},{18,26},{... | collective-permute-start | bytes 196616 | tf_op jit(solution)/shard_map/ppermute | solution.py:21
  11.5 95.6 %collective-permute-start.1 = (f32[16,256]{1,0:T(8,128)S(1)}, f32[16,256]{1,0:T(8,128)S(1)}, u32[]{:S(2)}, u32[]{:S(2)}) collective-permute-start(f32[16,256]{1,0:T(8,128)S(1)} %bitcast.415), channel_id=1, source_target_pairs={{0,1},{1,2},{2,3},{3,4},{4,5},{5,6},{6,7},{8,9},{9,10},{10,11},{11... | collective-permute-start | bytes 49160 | tf_op jit(solution)/shard_map/ppermute | solution.py:21
  17.3 101.9 %collective-permute-start.3 = (f32[1,64,256]{2,1,0:T(8,128)}, f32[1,64,256]{2,1,0:T(8,128)S(1)}, u32[]{:S(2)}, u32[]{:S(2)}) collective-permute-start(f32[1,64,256]{2,1,0:T(8,128)} %get-tuple-element.72), channel_id=1, source_target_pairs={{0,8},{8,16},{16,24},{1,9},{9,17},{17,25},{2,10},{10,18},{18,26},{... | collective-permute-start | bytes 196616 | tf_op jit(solution)/shard_map/ppermute | solution.py:29
  20.7 98.7 %collective-permute-start.2 = (f32[1,64,256]{2,1,0:T(8,128)}, f32[1,64,256]{2,1,0:T(8,128)S(1)}, u32[]{:S(2)}, u32[]{:S(2)}) collective-permute-start(f32[1,64,256]{2,1,0:T(8,128)} %get-tuple-element.71), channel_id=1, source_target_pairs={{8,0},{16,8},{24,16},{9,1},{17,9},{25,17},{10,2},{18,10},{26,18},{... | collective-permute-start | bytes 196616 | tf_op jit(solution)/shard_map/ppermute | solution.py:32
  28.9 13.8 %all-to-all-start = ((s32[32,1,32]{2,1,0:T(1,128)}), s32[32,1,32]{2,1,0:T(1,128)S(1)}, u32[]{:S(2)}, u32[]{:S(2)}) async-start(s32[32,1,32]{2,1,0:T(1,128)} %all_to_all.30), calls=%async_computation | async-start | bytes 32768 | tf_op jit(solution)/shard_map/all_to_all | solution.py:116
  49.7 40.0 %all-to-all-start.1 = ((f32[32,1,32]{2,1,0:T(1,128)}), f32[32,1,32]{2,1,0:T(1,128)S(1)}, u32[]{:S(2)}, u32[]{:S(2)}) async-start(f32[32,1,32]{2,1,0:T(1,128)} %all_to_all.32), calls=%async_computation.1 | async-start | bytes 32768 | tf_op jit(solution)/shard_map/all_to_all | solution.py:159
  96.3 12.5 %all-to-all-start.2 = ((f32[32,1,32]{2,1,0:T(1,128)}), f32[32,1,32]{2,1,0:T(1,128)S(1)}, u32[]{:S(2)}, u32[]{:S(2)}) async-start(f32[32,1,32]{2,1,0:T(1,128)} %all_to_all.34), calls=%async_computation.2 | async-start | bytes 32768 | tf_op jit(solution)/shard_map/all_to_all | solution.py:175
  101.8 126.8 %all-gather.5.cloned.1.call-start = ((), (), s32[]{:S(2)}) async-start(), calls=%async_computation.5 | async-start | bytes 1081344 | tf_op jit(solution)/shard_map/all_gather | solution.py:14
  121.0 8.7 collective-permute-start.5
  123.8 5.9 collective-permute-start.4
  137.2 6.4 collective-permute-start.6
  138.5 5.1 collective-permute-start.7
  143.7 7.2 collective-permute-start.9
  148.2 6.2 collective-permute-start.8
  163.7 62.2 %collective-permute-start.10 = (f32[1,64,256]{2,1,0:T(8,128)S(1)}, f32[1,64,256]{2,1,0:T(8,128)S(1)}, u32[]{:S(2)}, u32[]{:S(2)}) collective-permute-start(f32[1,64,256]{2,1,0:T(8,128)S(1)} %get-tuple-element.68), channel_id=1, source_target_pairs={{8,0},{16,8},{24,16},{9,1},{17,9},{25,17},{10,2},{18,10},{26,18},{... | collective-permute-start | bytes 196616 | tf_op jit(solution)/shard_map/ppermute | solution.py:32
  165.0 60.9 %collective-permute-start.11 = (f32[1,64,256]{2,1,0:T(8,128)S(1)}, f32[1,64,256]{2,1,0:T(8,128)S(1)}, u32[]{:S(2)}, u32[]{:S(2)}) collective-permute-start(f32[1,64,256]{2,1,0:T(8,128)S(1)} %get-tuple-element.67), channel_id=1, source_target_pairs={{0,8},{8,16},{16,24},{1,9},{9,17},{17,25},{2,10},{10,18},{18,26},{... | collective-permute-start | bytes 196616 | tf_op jit(solution)/shard_map/ppermute | solution.py:29
  177.4 45.5 %all-to-all-start.3 = ((f32[32,1,32]{2,1,0:T(1,128)}), f32[32,1,32]{2,1,0:T(1,128)S(1)}, u32[]{:S(2)}, u32[]{:S(2)}) async-start(f32[32,1,32]{2,1,0:T(1,128)} %all_to_all.36), calls=%async_computation.3 | async-start | bytes 32768 | tf_op jit(solution)/shard_map/all_to_all | solution.py:159
  225.9 338.0 %collective-permute-start.13 = (f32[18,1,256]{2,1,0:T(1,128)S(1)}, f32[18,1,256]{2,1,0:T(1,128)S(1)}, u32[]{:S(2)}, u32[]{:S(2)}) collective-permute-start(f32[18,1,256]{2,1,0:T(1,128)S(1)} %get-tuple-element.60), channel_id=1, source_target_pairs={{0,1},{1,2},{2,3},{3,4},{4,5},{5,6},{6,7},{8,9},{9,10},{10,11},{11... | collective-permute-start | bytes 55304 | tf_op jit(solution)/shard_map/ppermute | solution.py:29
  227.2 336.7 %collective-permute-start.12 = (f32[18,1,256]{2,1,0:T(1,128)S(1)}, f32[18,1,256]{2,1,0:T(1,128)S(1)}, u32[]{:S(2)}, u32[]{:S(2)}) collective-permute-start(f32[18,1,256]{2,1,0:T(1,128)S(1)} %get-tuple-element.59), channel_id=1, source_target_pairs={{1,0},{2,1},{3,2},{4,3},{5,4},{6,5},{7,6},{9,8},{10,9},{11,10},{12... | collective-permute-start | bytes 55304 | tf_op jit(solution)/shard_map/ppermute | solution.py:32
  542.5 10.4 %all-to-all-start.4 = ((f32[32,1,32]{2,1,0:T(1,128)}), f32[32,1,32]{2,1,0:T(1,128)S(1)}, u32[]{:S(2)}, u32[]{:S(2)}) async-start(f32[32,1,32]{2,1,0:T(1,128)} %all_to_all.38), calls=%async_computation.4 | async-start | bytes 32768 | tf_op jit(solution)/shard_map/all_to_all | solution.py:175
  545.8 85.0 %all-gather.7.cloned.1.call-start = ((), (), s32[]{:S(2)}) async-start(), calls=%async_computation.6 | async-start | bytes 1081344 | tf_op jit(solution)/shard_map/all_gather | solution.py:14
  572.8 6.2 collective-permute-start.14
  579.0 42.7 %collective-permute-start.17 = (f32[18,1,256]{2,1,0:T(1,128)S(1)}, f32[18,1,256]{2,1,0:T(1,128)S(1)}, u32[]{:S(2)}, u32[]{:S(2)}) collective-permute-start(f32[18,1,256]{2,1,0:T(1,128)S(1)} %get-tuple-element.58), channel_id=1, source_target_pairs={{0,1},{1,2},{2,3},{3,4},{4,5},{5,6},{6,7},{8,9},{9,10},{10,11},{11... | collective-permute-start | bytes 55304 | tf_op jit(solution)/shard_map/ppermute | solution.py:29
  581.8 39.9 %collective-permute-start.16 = (f32[18,1,256]{2,1,0:T(1,128)S(1)}, f32[18,1,256]{2,1,0:T(1,128)S(1)}, u32[]{:S(2)}, u32[]{:S(2)}) collective-permute-start(f32[18,1,256]{2,1,0:T(1,128)S(1)} %get-tuple-element.57), channel_id=1, source_target_pairs={{1,0},{2,1},{3,2},{4,3},{5,4},{6,5},{7,6},{9,8},{10,9},{11,10},{12... | collective-permute-start | bytes 55304 | tf_op jit(solution)/shard_map/ppermute | solution.py:32
  (23 other events, 596.4 us)
Sparse Core Ops, SparseCore 0:
  107.2 55.3 all-gather.4
  550.5 55.2 all-gather.6
